TPU v7x, 256 devices: a whole 4x4x8 slice. The times are simulated.
256 devices in a mesh: ctx: 32 (over z_lo, x, y), fsdp: 8 (over z_hi, core).
Axes of the slice: x: 4, y: 4, z: 8 (z_hi: 4, z_lo: 2; z = z_hi * 2 + z_lo), core: 2. Of those that a mesh axis runs over, the one named last changes fastest.
Arguments:
- tokens: bfloat16 [8, 4096, 4096], P('fsdp', 'ctx'), may hold values from -6 to 6
- positions: int32 [8, 4096], P('fsdp', 'ctx'), may hold values from 0 to 4095, as said below
- norm_gain: float32 [4096], replicated, may hold values from 0.5 to 1.5
- query_weight: bfloat16 [4096, 2048], P('fsdp'), may hold values from -1 to 1
- key_weight: bfloat16 [4096, 512], P('fsdp'), may hold values from -1 to 1
- value_matrix: bfloat16 [4096, 512], P('fsdp'), may hold values from -0.09375 to 0.09375
Outputs:
- attended: bfloat16 [8, 4096, 2048], P('fsdp', 'ctx')
Inputs may be any that keep to these rules, and one draw needn't show every extreme that they name: In each sequence every position from 0 to 4095 appears once, in runs of 64 consecutive rising positions that begin at multiples of 64 in the array.
All inputs are finite; a program needn't handle non-finite values.
Results may differ from a plain program's by a relative error of at most 0.012.
The roundings to bfloat16 on the way count: a program that leaves them out, or rounds other values in their place, can miss the bound.
Values may be sent and summed in bfloat16 or wider, within the bound.
A program may use at most 128 MiB of HBM per device.

v0:
```python
import jax
import jax.numpy as jnp
from jax import lax
from jax.sharding import PartitionSpec as P

QUERY_HEADS = 16
KEY_VALUE_HEADS = 4
HEAD_SIZE = 128


EPS = 1e-05
BASE = 500000.0
MASK_FLOOR = -1e30


def joined_along(parts, dim):
    parts = jnp.moveaxis(parts, 0, dim)
    shape = parts.shape
    return parts.reshape(*shape[:dim], shape[dim] * shape[dim + 1], *shape[dim + 2 :])


def copy_for_each(shard, axis):
    size = lax.axis_size(axis)
    return lax.all_to_all(
        jnp.broadcast_to(shard[None], (size, *shard.shape)), axis, 0, 0, tiled=True
    )


def gathered_copies(shard, axis, dim):
    return joined_along(copy_for_each(shard, axis), dim)


def side_by_side(arrays, axis, dim, along):
    ends, at = ([], 0)
    for a in arrays[:-1]:
        at += a.shape[along]
        ends.append(at)
    both = jnp.concatenate(arrays, axis=along)
    return tuple(jnp.split(lax.all_gather(both, axis, axis=dim, tiled=True), ends, axis=along))


def normalize(tokens, norm_gain):
    values = tokens.astype(jnp.float32)
    inverse = lax.rsqrt(jnp.mean(values * values, axis=-1, keepdims=True) + EPS)
    return (values * inverse * norm_gain).astype(jnp.bfloat16)


def rope_tables(places, head_dim):
    half_dim = head_dim // 2
    frequency = BASE ** (-(jnp.arange(half_dim, dtype=jnp.float32) * 2.0) / head_dim)
    angles = places.astype(jnp.float32)[:, None] * frequency[None, :]
    return (jnp.cos(angles), jnp.sin(angles))


def apply_rotation(x, cosine_table_rows, sine_table_rows):
    half_dim = x.shape[-1] // 2
    first_half = x[..., :half_dim]
    second_half = x[..., half_dim:]
    cosine_part = cosine_table_rows[:, None, :]
    sine_part = sine_table_rows[:, None, :]
    return jnp.concatenate(
        [
            first_half * cosine_part - second_half * sine_part,
            second_half * cosine_part + first_half * sine_part,
        ],
        axis=-1,
    )


def on_device(tokens, positions, norm_gain, query_weight, key_weight, value_matrix):
    normed = normalize(tokens[0], norm_gain)
    token_row_block = normed.shape[0]
    query_width = query_weight.shape[1]
    key_width = key_weight.shape[1]
    query_groups = QUERY_HEADS // KEY_VALUE_HEADS
    places = positions[0]
    all_places = gathered_copies(places, "ctx", 0)
    pieces = side_by_side((query_weight, key_weight, value_matrix), "fsdp", 0, 1)
    portion_rows = pieces[0].shape[0]
    query_flat, key_flattened, value_flat = tuple(
        (jnp.dot(normed, piece, preferred_element_type=jnp.float32) for piece in pieces)
    )
    cosine_table_rows, sine_table_rows = rope_tables(places, HEAD_SIZE)
    grouped_query = (
        apply_rotation(
            query_flat.reshape(token_row_block, QUERY_HEADS, HEAD_SIZE),
            cosine_table_rows,
            sine_table_rows,
        )
        .astype(jnp.bfloat16)
        .reshape(token_row_block, KEY_VALUE_HEADS, query_groups, HEAD_SIZE)
    )
    key_part = (
        apply_rotation(
            key_flattened.reshape(token_row_block, KEY_VALUE_HEADS, HEAD_SIZE),
            cosine_table_rows,
            sine_table_rows,
        )
        .astype(jnp.bfloat16)
        .reshape(token_row_block, key_width)
    )
    value_part = value_flat.astype(jnp.bfloat16)
    start_state = (
        jnp.full((token_row_block, KEY_VALUE_HEADS, query_groups), MASK_FLOOR, jnp.float32),
        jnp.zeros((token_row_block, KEY_VALUE_HEADS, query_groups), jnp.float32),
        jnp.zeros((token_row_block, KEY_VALUE_HEADS, query_groups, HEAD_SIZE), jnp.float32),
    )

    def attend(running, key_portion, value_portion, key_places):
        maximum, denominator, accum = running
        portion_rows = key_portion.shape[0]
        key_head_split = key_portion.reshape(portion_rows, KEY_VALUE_HEADS, HEAD_SIZE)
        value_head_split = value_portion.reshape(portion_rows, KEY_VALUE_HEADS, HEAD_SIZE)
        scores = jnp.einsum(
            "qhgd,khd->qhgk", grouped_query, key_head_split, preferred_element_type=jnp.float32
        ) * HEAD_SIZE ** (-0.5)
        allowed = (key_places[None, :] <= places[:, None])[:, None, None, :]
        scores = jnp.where(allowed, scores, MASK_FLOOR)
        new_max = jnp.maximum(maximum, jnp.max(scores, axis=-1))
        weights = jnp.where(allowed, jnp.exp(scores - new_max[..., None]), 0.0)
        factor = jnp.exp(maximum - new_max)
        denominator = denominator * factor + jnp.sum(weights, axis=-1)
        rounded = weights.astype(jnp.bfloat16)
        accum = accum * factor[..., None] + jnp.einsum(
            "qhgk,khd->qhgd", rounded, value_head_split, preferred_element_type=jnp.float32
        )
        return (new_max, denominator, accum)

    key_whole, value_whole = side_by_side((key_part, value_part), "ctx", 0, 1)
    key_count = key_whole.shape[0]
    block_size = min(512, key_count)
    block_count = key_count // block_size

    def scan_block(running, pieces):
        return (attend(running, pieces[0], pieces[1], pieces[2]), None)

    finished, unused = lax.scan(
        scan_block,
        start_state,
        (
            key_whole.reshape(block_count, block_size, key_width),
            value_whole.reshape(block_count, block_size, key_width),
            all_places.reshape(block_count, block_size),
        ),
    )
    maximum, denominator, accum = finished
    attended = (
        (accum / denominator[..., None])
        .astype(jnp.bfloat16)
        .reshape(1, token_row_block, query_width)
    )
    return attended


def solution(mesh):
    placed = (
        P("fsdp", "ctx", None),
        P("fsdp", "ctx"),
        P(),
        P("fsdp", None),
        P("fsdp", None),
        P("fsdp", None),
    )
    return jax.shard_map(
        on_device, mesh=mesh, in_specs=placed, out_specs=P("fsdp", "ctx", None), check_vma=False
    )
```

profile of v0, /device:TPU:8, one launch (start us, length us, event | category | flops | bytes accessed | tf_op | source)
XLA Modules:
  0.0 480.2 jit_solution(3413744317841895253)
XLA Ops:
  6.5 3.4 pad_maximum_fusion
  10.5 229.3 %all-gather.3.cloned.1.call-done = bf16[4096,3072]{1,0:T(8,128)(2,1)} async-done(((bf16[512,3072]{1,0:T(8,128)(2,1)}), bf16[4096,3072]{1,0:T(8,128)(2,1)}) %all-gather.3.cloned.1.call-update) | async-done | bytes 25165840 | tf_op jit(solution)/shard_map/all_gather | solution.py:39
  239.8 4.4 slice_bitcast_fusion.1
  244.2 6.4 %copy.27 = bf16[512,4096]{1,0:T(8,128)(2,1)} copy(bf16[512,4096]{0,1:T(8,128)(2,1)} %slice_bitcast_fusion.1) | data formatting | bytes 8388608 | tf_op jit(solution)/shard_map/dot_general | solution.py:81
  250.6 3.5 fusion.34
  254.3 2.9 fusion.25
  257.3 0.7 pad_maximum_fusion.2
  258.6 7.4 %all-to-all-start = ((s32[32,1,128]{2,1,0:T(1,128)}), s32[32,1,128]{2,1,0:T(1,128)S(1)}, u32[]{:S(2)}, u32[]{:S(2)}) async-start(s32[32,1,128]{2,1,0:T(1,128)} %broadcast_in_dim.48), calls=%async_computation | async-start | bytes 32768 | tf_op jit(solution)/shard_map/all_to_all | solution.py:24
  266.1 7.1 %all-to-all-done = s32[32,1,128]{2,1,0:T(1,128)S(1)} async-done(((s32[32,1,128]{2,1,0:T(1,128)}), s32[32,1,128]{2,1,0:T(1,128)S(1)}, u32[]{:S(2)}, u32[]{:S(2)}) %all-to-all-start) | async-done | bytes 16416 | tf_op jit(solution)/shard_map/all_to_all | solution.py:24
  274.4 14.1 %slice_bitcast_fusion = bf16[2048,4096]{0,1:T(8,128)(2,1)} fusion(bf16[4096,3072]{1,0:T(8,128)(2,1)} %all-gather.3.cloned.1.call-done), kind=kLoop, calls=%fused_computation.21 | loop fusion | bytes 33554432 | tf_op jit(solution)/shard_map/dot_general | solution.py:81
  288.5 20.8 %copy.29 = bf16[2048,4096]{1,0:T(8,128)(2,1)} copy(bf16[2048,4096]{0,1:T(8,128)(2,1)} %slice_bitcast_fusion) | data formatting | bytes 33554432 | tf_op jit(solution)/shard_map/dot_general | solution.py:81
  309.3 8.3 %fusion.32 = f32[128,16,128]{0,2,1:T(8,128)S(1)} fusion(bf16[16,128,4096]{2,1,0:T(8,128)(2,1)} %bitcast.90, bf16[1,128,4096]{2,1,0:T(8,128)(2,1)S(1)} %copy-done, f32[4096]{0:T(1024)S(1)} %copy-done.2, f32[128]{0:T(128)S(1)} %add_rsqrt_fusion), kind=kOutput, calls=%fused_computation.43 | convolution fusion | flops 2149580800 | bytes 18891264 | tf_op jit(solution)/shard_map/dot_general | solution.py:81
  318.6 106.1 %all-gather.5.cloned.1.call-done = bf16[4096,1024]{1,0:T(8,128)(2,1)} async-done(((bf16[128,1024]{1,0:T(8,128)(2,1)}), bf16[4096,1024]{1,0:T(8,128)(2,1)}) %all-gather.5.cloned.1.call-update) | async-done | bytes 8388624 | tf_op jit(solution)/shard_map/all_gather | solution.py:39
  424.7 5.7 %fusion.36 = (bf16[4096,512]{1,0:T(8,128)(2,1)}, bf16[4096,512]{1,0:T(8,128)(2,1)}) fusion(bf16[4096,1024]{1,0:T(8,128)(2,1)} %all-gather.5.cloned.1.call-done), kind=kLoop, calls=%fused_computation.54 | loop fusion | bytes 16777216 | tf_op jit(solution)/shard_map/split | solution.py:39
  430.5 41.7 %while.15 = (s32[]{:T(128)}, f32[128,4,4]{0,2,1:T(4,128)S(1)}, f32[128,4,4]{0,2,1:T(4,128)S(1)}, f32[128,4,4,128]{0,3,2,1:T(8,128)S(1)}, s32[8,512]{1,0:T(8,128)...) while((s32[]{:T(128)}, f32[128,4,4]{0,2,1:T(4,128)S(1)}, ...), condition=%wide.region_4.5_spmd.clone, body=%wide.region_1.4_spmd.clone.sunk | while | flops 551364608 | bytes 20847240 | solution.py:137
  430.6 1.3 constant_dynamic-slice_fusion.6
  432.4 0.9 fusion.54
  433.2 1.0 fusion.55
  434.3 1.4 fusion.57
  435.8 1.3 constant_dynamic-slice_fusion.6
  437.6 0.9 fusion.54
  438.4 1.0 fusion.55
  439.5 1.4 fusion.57
  441.1 1.3 constant_dynamic-slice_fusion.6
  442.8 0.9 fusion.54
  443.6 1.0 fusion.55
  444.7 1.4 fusion.57
  446.3 1.3 constant_dynamic-slice_fusion.6
  448.0 0.9 fusion.54
  448.9 1.0 fusion.55
  449.9 1.4 fusion.57
  451.5 1.3 constant_dynamic-slice_fusion.6
  453.2 0.9 fusion.54
  454.1 1.0 fusion.55
  455.1 1.4 fusion.57
  456.7 1.3 constant_dynamic-slice_fusion.6
  458.4 0.9 fusion.54
  459.3 1.0 fusion.55
  460.4 1.4 fusion.57
  461.9 1.3 constant_dynamic-slice_fusion.6
  463.6 0.9 fusion.54
  464.5 1.0 fusion.55
  465.6 1.4 fusion.57
  467.1 1.3 constant_dynamic-slice_fusion.6
  468.8 0.9 fusion.54
  469.7 1.0 fusion.55
  470.8 1.4 fusion.57
  472.3 1.0 copy.38
  (86 shorter events, 8.5 us)
Async XLA Ops:
  6.5 3.5 copy-start
  6.5 3.7 copy-start.1
  6.5 233.2 %all-gather.3.cloned.1.call-start = ((), (), s32[]{:S(2)}) async-start(), calls=%async_computation.1 | async-start | bytes 28311552 | tf_op jit(solution)/shard_map/all_gather | solution.py:39
  9.9 414.8 %all-gather.5.cloned.1.call-start = ((), (), s32[]{:S(2)}) async-start(), calls=%async_computation.2 | async-start | bytes 8650752 | tf_op jit(solution)/shard_map/all_gather | solution.py:39
  244.2 6.4 %copy-start.2 = (f32[4096]{0:T(1024)S(1)}, f32[4096]{0:T(1024)}, u32[]{:S(2)}) copy-start(f32[4096]{0:T(1024)} %param.10) | copy-start | bytes 49156
  258.6 14.5 %all-to-all-start = ((s32[32,1,128]{2,1,0:T(1,128)}), s32[32,1,128]{2,1,0:T(1,128)S(1)}, u32[]{:S(2)}, u32[]{:S(2)}) async-start(s32[32,1,128]{2,1,0:T(1,128)} %broadcast_in_dim.48), calls=%async_computation | async-start | bytes 32768 | tf_op jit(solution)/shard_map/all_to_all | solution.py:24
Sparse Core Ops, SparseCore 0:
  10.0 229.7 all-gather.2
  258.1 166.5 all-gather.4
where the time goes:
time: 481 us; the launch traced here: 480 us
  waiting for transfers between devices  343 us (71%)
  local copies, waits for them, and re-layouts  68 us (14%)
  matrix products  32.5 us (7%)
  other arithmetic  15.5 us (3%)
  between operations  13.6 us (3%)
  starting transfers between devices  7.44 us (2%)
    all_gather x2, waiting for transfers between devices, side_by_side(): lax.all_gather(both, axis, axis=dim, tiled=True)  335 us
    dot_general x4, local copies, waits for them, and re-layouts, on_device(): jnp.dot(normed, piece, preferred_element_type=jnp.float32)  45.7 us
    dot_general x3, matrix products, on_device(): jnp.dot(normed, piece, preferred_element_type=jnp.float32)  14.7 us
    dynamic_slice x32, local copies, waits for them, and re-layouts, on_device(): lax.scan(scan_block, start_state, (key_whole.reshape(block_count, block_s...  13.7 us
    dot_general x8, matrix products, attend(): jnp.einsum('qhgk,khd->qhgd', rounded, value_head_split, preferred_element...  10.9 us
  transfers between devices with their start and end apart: 3, of which 3 were waited for; matrix products, arithmetic and copies ran while one was open for 10% of the time, Pallas kernels for 0%

commit v1 on v0

v1 whole, which is shorter than its diff:
```python
import math

import jax
import jax.numpy as jnp
from jax import lax
from jax.experimental import pallas as pl
from jax.experimental.pallas import tpu as pltpu
from jax.sharding import PartitionSpec as P

HEAD = 128
GROUP = 4
EPS = 1e-05
BASE = 500000.0
FLOOR = -1e30
LOG2E = math.log2(math.e)
F32, BF16 = jnp.float32, jnp.bfloat16


def rope_tables(places):
    half = HEAD // 2
    frequency = BASE ** (-(jnp.arange(half, dtype=F32) * 2.0) / HEAD)
    angles = places.astype(F32)[:, None] * frequency[None, :]
    return jnp.concatenate([jnp.cos(angles), jnp.sin(angles)], axis=1)


def around(n):
    return jnp.where(n == 0, 0, jnp.where(n == 1, 3, jnp.where(n == 2, 1, 2)))


class PlaneGather:
    def __init__(self, at, piece, send_sem, recv_sem):
        self.at, self.piece, self.ss, self.rs = at, piece, send_sem, recv_sem

    def slot(self, g, da, db):
        dx, dy = (da, db) if g == 0 else (db, da)
        return lax.rem(self.at["x"] + dx, 4) * 4 + lax.rem(self.at["y"] + dy, 4)

    def neighbour(self, g, axis, step):
        along_x = (axis == 0) == (g == 0)
        dx, dy = (step, 0) if along_x else (0, step)
        ctx = self.at["zl"] * 16 + lax.rem(self.at["x"] + dx, 4) * 4 + lax.rem(self.at["y"] + dy, 4)
        return {"ctx": ctx, "fsdp": self.at["f"]}

    def copy(self, g, n, h, p, device):
        ref = self.piece(g, h, p)
        return pltpu.make_async_remote_copy(
            src_ref=ref, dst_ref=ref, send_sem=self.ss.at[g, n], recv_sem=self.rs.at[g, p, h],
            device_id=device, device_id_type=pl.DeviceIdType.MESH)

    def send(self, g, n, h, p, axis, step):
        self.copy(g, n, h, p, self.neighbour(g, axis, step)).start()

    def arrived(self, g, h, p):
        self.copy(g, 0, h, p, self.neighbour(g, 0, 1)).wait_recv()

    def second(self, g, n, da):
        p = self.slot(g, da, 0)
        for h in (0, 1):
            self.send(g, 6 + n * 6 + 2 * h, h, p, 1, 1)
            self.send(g, 6 + n * 6 + 2 * h + 1, h, p, 1, 3)

    def s0(self, g):
        p = self.slot(g, 0, 0)
        for h in (0, 1):
            self.send(g, 2 * h, h, p, 0, 1)
            self.send(g, 2 * h + 1, h, p, 0, 3)
        self.second(g, 0, 0)

    def s1(self, g):
        for n, d, h, step in ((1, 3, 0, 1), (2, 1, 1, 3)):
            p = self.slot(g, d, 0)
            self.arrived(g, h, p)
            self.send(g, 3 + n, h, p, 0, step)
            self.arrived(g, 1 - h, p)
            self.second(g, n, d)

    def s2(self, g):
        p = self.slot(g, 2, 0)
        for h in (0, 1):
            self.arrived(g, h, p)
        self.second(g, 3, 2)

    def s3(self, g, n):
        d = around(n)
        for db, h, step in ((3, 0, 1), (1, 1, 3)):
            p = self.slot(g, d, db)
            self.arrived(g, h, p)
            self.send(g, 6 + n * 6 + 4 + h, h, p, 1, step)
        for db, h in ((3, 1), (1, 0)):
            self.arrived(g, h, self.slot(g, d, db))

    def s4(self, g, n):
        for h in (0, 1):
            self.arrived(g, h, self.slot(g, around(n), 2))

    def finish(self):
        for g in (0, 1):
            for n in range(30):
                self.copy(g, n, 0, 0, self.neighbour(g, 0, 1)).wait_send()


def rotate(u, table):
    turned = pltpu.roll(table, 64, 1)
    first = lax.broadcasted_iota(jnp.int32, table.shape, 1) < 64
    cosine = jnp.where(first, table, turned)
    sine = jnp.where(first, -turned, table)
    return u * cosine + pltpu.roll(u, 64, 1) * sine


def kernel(tok, gain, cs, qw, kw, vw, out, tq, csq, wkv, wq, kvb, qt, acc, top, proj, osend, obuf,
           loc_s, zs, zr, ws, wr, ts, tr, fs, fr, s_a, r_a, s_b, r_b, s_c, r_c, os_, or_, outs_):
    c, f = lax.axis_index("ctx"), lax.axis_index("fsdp")
    zl, x, y = c // 16, lax.rem(c // 4, 4), lax.rem(c, 4)
    zh, k = f // 2, lax.rem(f, 2)
    col = x * 4 + y
    at = {"zl": zl, "x": x, "y": y, "f": f}
    mine, head = k * 2 + zl, zl * 2 + k

    def device(zh_, zl_, k_):
        return {"ctx": zl_ * 16 + col, "fsdp": zh_ * 2 + k_}

    def remote(src, dst, ss, rs, dev):
        return pltpu.make_async_remote_copy(src_ref=src, dst_ref=dst, send_sem=ss, recv_sem=rs, device_id=dev,
                                            device_id_type=pl.DeviceIdType.MESH)

    core = device(zh, zl, 1 - k)
    chip = device(zh, 1 - zl, k)
    diagonal = device(zh, 1 - zl, 1 - k)
    step_a = 1 + 2 * zl
    slab_a = lax.rem(zh + 4 - step_a, 4)
    slab_c = lax.rem(zh + step_a, 4)
    slab_b = lax.rem(zh + 2, 4)
    push_to = [(step_a, slab_a, zl_, k_) for zl_ in (0, 1) for k_ in (0, 1)] + [(2, slab_b, 1 - zl, k_) for k_ in (0, 1)]

    barrier = pltpu.get_barrier_semaphore()
    ring = PlaneGather(at, None, None, None)
    friends = [core, chip, diagonal]
    friends += [ring.neighbour(0, axis, step) for axis in (0, 1) for step in (1, 3)]
    friends += [device(slab_a, zl_, k_) for zl_ in (0, 1) for k_ in (0, 1)]
    friends += [device(slab_b, 1 - zl, k_) for k_ in (0, 1)]
    friends += [device(slab_c, zl, k_) for k_ in (0, 1)]
    for friend in friends:
        pl.semaphore_signal(barrier, inc=1, device_id=friend, device_id_type=pl.DeviceIdType.MESH)

    own = [
        pltpu.make_async_copy(kw.at[:, pl.ds(pl.multiple_of(head * 128, 128), 128)], wkv.at[k, :, pl.ds(0, 128)], loc_s.at[0]),
        pltpu.make_async_copy(vw.at[:, pl.ds(pl.multiple_of(head * 128, 128), 128)], wkv.at[k, :, pl.ds(128, 128)], loc_s.at[1]),
        pltpu.make_async_copy(qw.at[:, pl.ds(pl.multiple_of(head * 512, 512), 512)], wq.at[k], loc_s.at[2]),
    ]
    for copy in own:
        copy.start()

    def norm_rows(i, _):
        rows = pl.ds(pl.multiple_of(i * 16, 16), 16)
        values = tok[rows, :].astype(F32)
        inverse = lax.rsqrt(jnp.mean(values * values, axis=-1, keepdims=True) + EPS)
        tq[mine, rows, :] = (values * inverse * gain[...]).astype(BF16)
        return 0

    lax.fori_loop(0, 8, norm_rows, 0)
    csq[mine] = cs[...]

    pl.semaphore_wait(barrier, len(friends))

    rows = pl.ds(pl.multiple_of(col * 32, 32), 32)

    def pushes(n, what):
        r, slab, zl_, k_ = push_to[n]
        j = zl_ * 2 + k_
        index = r * 2 + k
        dev = device(slab, zl_, k_)
        narrow = pl.ds(pl.multiple_of(j * 128, 128), 128)
        wide = pl.ds(pl.multiple_of(j * 512, 512), 512)
        src, dst = (
            (kw.at[rows, narrow], wkv.at[index, rows, pl.ds(0, 128)]),
            (vw.at[rows, narrow], wkv.at[index, rows, pl.ds(128, 128)]),
            (qw.at[rows, wide], wq.at[index, rows, :]),
        )[what]
        return remote(src, dst, zs.at[n, what], zr.at[index - 2, what], dev)

    def pulled(i, what):
        dst = (wkv.at[2 + i, rows, pl.ds(0, 128)], wkv.at[2 + i, rows, pl.ds(128, 128)], wq.at[2 + i, rows, :])[what]
        return remote(dst, dst, zs.at[0, what], zr.at[i, what], core)

    for what in (0, 1, 2):
        for n in range(6):
            pushes(n, what).start()

    other = zl * 2 + (1 - k)
    to_core = [
        remote(kw.at[:, pl.ds(pl.multiple_of(other * 128, 128), 128)], wkv.at[k, :, pl.ds(0, 128)], ws.at[0], wr.at[0], core),
        remote(vw.at[:, pl.ds(pl.multiple_of(other * 128, 128), 128)], wkv.at[k, :, pl.ds(128, 128)], ws.at[1], wr.at[1], core),
        remote(qw.at[:, pl.ds(pl.multiple_of(other * 512, 512), 512)], wq.at[k], ws.at[2], wr.at[2], core),
        remote(tq.at[mine], tq.at[mine], ws.at[3], wr.at[3], core),
        remote(cs, csq.at[mine], ws.at[4], wr.at[4], core),
    ]
    for copy in to_core:
        copy.start()

    def quarter(q, i):
        return tq.at[q, :, pl.ds(i * 1024, 1024)]

    def to_chip(i):
        if i == 0:
            return remote(cs, csq.at[mine], ts.at[0], tr.at[0], chip)
        return remote(quarter(mine, i - 1), quarter(mine, i - 1), ts.at[i], tr.at[i], chip)

    theirs = k * 2 + (1 - zl)

    def from_chip(i):
        ref = csq.at[theirs] if i == 0 else quarter(theirs, i - 1)
        return remote(ref, ref, ts.at[i], tr.at[i], chip)

    def onward(i):
        ref = csq.at[theirs] if i == 0 else quarter(theirs, i - 1)
        return remote(ref, ref, fs.at[i], fr.at[i], core)

    far = (1 - k) * 2 + (1 - zl)

    def handed(i):
        ref = csq.at[far] if i == 0 else quarter(far, i - 1)
        return remote(ref, ref, fs.at[i], fr.at[i], core)

    for i in range(5):
        to_chip(i).start()

    wkv_g = PlaneGather(at, lambda g, h, p: wkv.at[pl.ds(2 + 3 * g, 3), pl.ds(pl.multiple_of(p * 32 + 16 * h, 16), 16), :],
                        s_a, r_a)
    wq_g = PlaneGather(at, lambda g, h, p: wq.at[pl.ds(2 + 3 * g, 3), pl.ds(pl.multiple_of(p * 32 + 16 * h, 16), 16), :],
                       s_b, r_b)
    kv_g = PlaneGather(at, lambda g, h, p: kvb.at[g, p, h], s_c, r_c)

    for i in range(6):
        pulled(i, 0).wait_recv()
        pulled(i, 1).wait_recv()
    for g in (0, 1):
        wkv_g.s0(g)
    for i in range(6):
        pulled(i, 2).wait_recv()
    for g in (0, 1):
        wq_g.s0(g)
    for g in (0, 1):
        wkv_g.s1(g)
    for g in (0, 1):
        wkv_g.s2(g)
    for g in (0, 1):
        wq_g.s1(g)

    def s3_kv(n, _):
        for g in (0, 1):
            wkv_g.s3(g, n)
        return 0

    lax.fori_loop(0, 4, s3_kv, 0)
    for g in (0, 1):
        wq_g.s2(g)

    def s4_kv(n, _):
        for g in (0, 1):
            wkv_g.s4(g, n)
        return 0

    lax.fori_loop(0, 4, s4_kv, 0)

    def s3_q(n, _):
        for g in (0, 1):
            wq_g.s3(g, n)
        return 0

    for i in range(5):
        if i < 2:
            from_chip(i).wait_recv()
            onward(i).start()
    lax.fori_loop(0, 2, s3_q, 0)
    for i in (2, 3):
        from_chip(i).wait_recv()
        onward(i).start()
    lax.fori_loop(2, 4, s3_q, 0)
    from_chip(4).wait_recv()
    onward(4).start()
    for copy in own:
        copy.wait()
    for copy in to_core:
        copy.wait_recv()
    for i in range(5):
        handed(i).wait_recv()

    def features(r):
        start = pl.multiple_of(lax.rem(zh + r, 4) * 1024, 1024)
        return tq[:, :, pl.ds(start, 1024)].reshape(512, 1024)

    def project_kv(r, _):
        w = wkv[pl.ds(2 * r, 2)].reshape(1024, 256)
        part = jnp.dot(features(r), w, preferred_element_type=F32)

        @pl.when(r == 0)
        def _():
            proj[:, 0:256] = part

        @pl.when(r > 0)
        def _():
            proj[:, 0:256] = proj[:, 0:256] + part

        return 0

    lax.fori_loop(0, 4, project_kv, 0)
    lane = lax.broadcasted_iota(jnp.int32, (1, 128), 1)
    offset = lax.rem(lane, 64).astype(F32)
    for g in (0, 1):
        for h in (0, 1):
            i = g * 2 + h
            key = rotate(proj[pl.ds(i * 128, 128), 0:128], csq[i, 0:128, :])
            kvb[g, col, h, 0:128, :] = key.astype(BF16)
            kvb[g, col, h, 128:256, :] = proj[pl.ds(i * 128, 128), 128:256].T.astype(BF16)
            block = (csq[i, 128:129, :] - offset) * (1.0 / 64.0)
            line = lax.broadcasted_iota(jnp.int32, (16, 128), 0)
            kvb[g, col, h, 256:272, :] = jnp.where(line == 0, jnp.broadcast_to(block, (16, 128)), 1.0).astype(BF16)
    for g in (0, 1):
        kv_g.s0(g)

    def s4_q(n, _):
        for g in (0, 1):
            wq_g.s4(g, n)
        return 0

    lax.fori_loop(0, 4, s4_q, 0)

    def project_q(r, _):
        w = wq[pl.ds(2 * r, 2)].reshape(1024, 512)
        part = jnp.dot(features(r), w, preferred_element_type=F32)

        @pl.when(r == 0)
        def _():
            proj[...] = part

        @pl.when(r > 0)
        def _():
            proj[...] = proj[...] + part

        return 0

    lax.fori_loop(0, 4, project_q, 0)
    for g in (0, 1):
        kv_g.s1(g)
    for i in range(4):
        for hd in range(GROUP):
            u = rotate(proj[pl.ds(i * 128, 128), pl.ds(hd * 128, 128)], csq[i, 0:128, :])
            at_col = ((i % 2) * GROUP + hd) * 128
            qt[i // 2, :, at_col:at_col + 128] = u.T.astype(BF16)
    acc[...] = jnp.zeros_like(acc)
    top[...] = jnp.full_like(top, FLOOR)

    scale = HEAD ** -0.5 * LOG2E
    within = lax.rem(lax.broadcasted_iota(jnp.int32, (128, 128), 0), 64).astype(F32)
    upper = lax.broadcasted_iota(jnp.int32, (128, 128), 0) < 64

    def attend(g, slots):
        keys, values, spots = [], [], []
        for p in slots:
            for h in (0, 1):
                keys.append(kvb[g, p, h, 0:128, :])
                values.append(kvb[g, p, h, 128:272, :])
                block = kvb[g, p, h, 256:272, :].astype(F32)[0:1, :]
                spots.append(jnp.where(upper, block[:, 0:1], block[:, 64:65]) * 64.0 + within)
        keys = jnp.concatenate(keys, axis=0)
        values = jnp.concatenate(values, axis=1)
        spots = jnp.concatenate(spots, axis=0)
        spots = jnp.concatenate([spots, spots], axis=1)
        for tile in range(4):
            cols = slice(tile * 256, tile * 256 + 256)
            place = csq[g * 2 + tile // 2, 128:129, :]
            place = jnp.concatenate([place, place], axis=1)
            scores = jnp.dot(keys, qt[g, :, cols], preferred_element_type=F32)
            scores = jnp.where(spots <= place, scores, FLOOR)
            before = top[g, 0:1, cols]
            now = jnp.maximum(before, jnp.max(scores, axis=0, keepdims=True))
            probs = jnp.exp2((scores - now) * scale).astype(BF16)
            factor = jnp.exp2((before - now) * scale)
            acc[g, :, cols] = acc[g, :, cols] * factor + jnp.dot(values, probs, preferred_element_type=F32)
            top[g, 0:1, cols] = now

    def round_(i, _):
        @pl.when(i == 1)
        def _():
            for g in (0, 1):
                kv_g.s2(g)

        @pl.when((i >= 2) & (i < 6))
        def _():
            for g in (0, 1):
                kv_g.s3(g, i - 2)

        @pl.when(i >= 6)
        def _():
            for g in (0, 1):
                kv_g.s4(g, (i - 6) * 2)
                kv_g.s4(g, (i - 6) * 2 + 1)

        n = lax.rem(i, 2) * 2
        da0 = around(jnp.where(i < 2, n, jnp.where(i < 6, i - 2, n)))
        da1 = around(jnp.where(i < 2, n + 1, jnp.where(i < 6, i - 2, n + 1)))
        db0 = jnp.where(i < 2, 0, jnp.where(i < 6, 3, 2))
        db1 = jnp.where(i < 2, 0, jnp.where(i < 6, 1, 2))
        for g in (0, 1):
            attend(g, (kv_g.slot(g, da0, db0), kv_g.slot(g, da1, db1)))
        return 0

    lax.fori_loop(0, 8, round_, 0)

    for g in (0, 1):
        for h in (0, 1):
            for hd in range(GROUP):
                at_col = (h * GROUP + hd) * 128
                one = acc[g, 0:128, at_col:at_col + 128] / acc[g, 129:130, at_col:at_col + 128]
                osend[g * 2 + h, :, hd * 128:hd * 128 + 128] = one.T.astype(BF16)

    def give(n):
        g, h, dev = ((k, 1 - zl, chip), (1 - k, 1 - zl, diagonal), (1 - k, zl, core))[n]
        return remote(osend.at[g * 2 + h], obuf.at[head], os_.at[n], or_.at[n], dev)

    def take(n):
        j = ((1 - zl) * 2 + k, (1 - zl) * 2 + 1 - k, zl * 2 + 1 - k)[n]
        return j, remote(obuf.at[j], obuf.at[j], os_.at[n], or_.at[n], core)

    for n in range(3):
        give(n).start()

    def store(src, j, n):
        return pltpu.make_async_copy(src, out.at[:, pl.ds(pl.multiple_of(j * 512, 512), 512)], outs_.at[n])

    last = [store(osend.at[mine], head, 3)]
    last[0].start()
    for n in (2, 0, 1):
        j, arrival = take(n)
        arrival.wait_recv()
        last.append(store(obuf.at[j], j, n))
        last[-1].start()
    for n in range(6):
        for what in (0, 1, 2):
            pushes(n, what).wait_send()
    for copy in to_core:
        copy.wait_send()
    for i in range(5):
        to_chip(i).wait_send()
        onward(i).wait_send()
    for gather in (wkv_g, wq_g, kv_g):
        gather.finish()
    for n in range(3):
        give(n).wait_send()
    for copy in last:
        copy.wait()


def on_device(tokens, positions, norm_gain, query_weight, key_weight, value_matrix):
    places = positions[0]
    table = jnp.concatenate([rope_tables(places), jnp.broadcast_to(places.astype(F32)[None, :], (8, 128))], axis=0)
    vmem = pl.BlockSpec(memory_space=pltpu.VMEM)
    anywhere = pl.BlockSpec(memory_space=pl.ANY)
    dma = pltpu.SemaphoreType.DMA
    result = pl.pallas_call(
        kernel,
        out_shape=jax.ShapeDtypeStruct((128, 2048), BF16),
        in_specs=[vmem, vmem, vmem, anywhere, anywhere, anywhere],
        out_specs=anywhere,
        scratch_shapes=[
            pltpu.VMEM((4, 128, 4096), BF16),
            pltpu.VMEM((4, 136, 128), F32),
            pltpu.VMEM((8, 512, 256), BF16),
            pltpu.VMEM((8, 512, 512), BF16),
            pltpu.VMEM((2, 16, 2, 272, 128), BF16),
            pltpu.VMEM((2, 128, 1024), BF16),
            pltpu.VMEM((2, 144, 1024), F32),
            pltpu.VMEM((2, 8, 1024), F32),
            pltpu.VMEM((512, 512), F32),
            pltpu.VMEM((4, 128, 512), BF16),
            pltpu.VMEM((4, 128, 512), BF16),
            dma((3,)), dma((6, 3)), dma((6, 3)), dma((5,)), dma((5,)), dma((5,)), dma((5,)), dma((5,)), dma((5,)),
            dma((2, 30)), dma((2, 16, 2)), dma((2, 30)), dma((2, 16, 2)), dma((2, 30)), dma((2, 16, 2)),
            dma((3,)), dma((3,)), dma((4,)),
        ],
        compiler_params=pltpu.CompilerParams(
            collective_id=0, has_side_effects=True, vmem_limit_bytes=56 * 1024 * 1024),
    )(tokens[0], norm_gain[None, :], table, query_weight, key_weight, value_matrix)
    return result[None]


def solution(mesh):
    placed = (
        P("fsdp", "ctx", None),
        P("fsdp", "ctx"),
        P(),
        P("fsdp", None),
        P("fsdp", None),
        P("fsdp", None),
    )
    return jax.shard_map(
        on_device, mesh=mesh, in_specs=placed, out_specs=P("fsdp", "ctx", None), check_vma=False
    )
```

time: 481 us -> 104 us (0.22)
  the two profiles are of different devices: /device:TPU:8 before, /device:TPU:1 now
where the time goes in v1:
time: 104 us
  Pallas kernels  100 us (96%)
  local copies, waits for them, and re-layouts  1.88 us (2%)
  other arithmetic  1.69 us (2%)
    pallas_call x1, Pallas kernels, on_device(): pl.pallas_call(kernel, out_shape=jax.ShapeDtypeStruct((128, 2048), BF16),...  100 us

profile of v1, /device:TPU:1, one launch (start us, length us, event | category | flops | bytes accessed | tf_op | source)
XLA Modules:
  0.0 103.9 jit_solution(12953579764920547623)
XLA Ops:
  0.0 0.7 convert_bitcast_fusion
  0.7 0.3 multiply_cosine_fusion
  1.0 0.7 pad_maximum_fusion.cs
  1.7 100.3 %shard_map.64 = bf16[128,2048]{1,0:T(8,128)(2,1)} custom-call(bf16[128,4096]{1,0:T(8,128)(2,1)} %bitcast.6, f32[1,4096]{1,0:T(1,128)} %bitcast.7, f32[136,128]{1,0:T(8,128)} %pad_maximum_fusion.cs, bf16[512,2048]{1,0:T(8,128)(2,1)} %qw.1, bf16[512,512]{1,0:T(8,128)(2,1)} %kw.1, bf16[512,512]{1,0:T(8,128)(2,1)} %vw.1), custom_call_target="tpu_custom_call" | custom-call | tf_op jit(solution)/shard_map/pallas_call | solution.py:460
  102.0 1.9 %copy.8 = bf16[1,128,2048]{2,1,0:T(8,128)(2,1)} copy(bf16[1,128,2048]{2,1,0:T(8,128)(2,1)} %bitcast.5) | data formatting | bytes 1048576
  (2 shorter events, 0.0 us)

commit v2 on v1

v2 whole, which is shorter than its diff:
```python
import math

import jax
import jax.numpy as jnp
from jax import lax
from jax.experimental import pallas as pl
from jax.experimental.pallas import tpu as pltpu
from jax.sharding import PartitionSpec as P

HEAD = 128
GROUP = 4
EPS = 1e-05
BASE = 500000.0
FLOOR = -1e30
LOG2E = math.log2(math.e)
F32, BF16 = jnp.float32, jnp.bfloat16


def rope_tables(places):
    half = HEAD // 2
    frequency = BASE ** (-(jnp.arange(half, dtype=F32) * 2.0) / HEAD)
    angles = places.astype(F32)[:, None] * frequency[None, :]
    return jnp.concatenate([jnp.cos(angles), jnp.sin(angles)], axis=1)


def around(n):
    return jnp.where(n == 0, 0, jnp.where(n == 1, 3, jnp.where(n == 2, 1, 2)))


class PlaneGather:
    def __init__(self, at, piece, sems, shared, sent):
        self.at, self.piece, self.sent = at, piece, sent
        self.send_sem, self.recv_sem, self.rest_sem, self.shared = *sems, shared

    def slot(self, g, da, db):
        dx, dy = (da, db) if g == 0 else (db, da)
        return lax.rem(self.at["x"] + dx, 4) * 4 + lax.rem(self.at["y"] + dy, 4)

    def neighbour(self, g, axis, step):
        along_x = (axis == 0) == (g == 0)
        dx, dy = (step, 0) if along_x else (0, step)
        ctx = self.at["zl"] * 16 + lax.rem(self.at["x"] + dx, 4) * 4 + lax.rem(self.at["y"] + dy, 4)
        return {"ctx": ctx, "fsdp": self.at["f"]}

    def early(self, g, d, h):
        return self.recv_sem.at[g, (0, 2, 4, 0)[d] + h] if d != 1 else self.recv_sem.at[g, 2 + h]

    def relayed(self, g, n, h):
        return self.recv_sem.at[g, 6 + n * 2 + h]

    def rest(self, n, h):
        return self.rest_sem.at[self.shared(n, h)]

    def copy(self, g, h, p, recv_sem, device):
        ref = self.piece(g, h, p)
        return pltpu.make_async_remote_copy(
            src_ref=ref, dst_ref=ref, send_sem=self.send_sem.at[min(h, self.send_sem.shape[0] - 1)], recv_sem=recv_sem,
            device_id=device, device_id_type=pl.DeviceIdType.MESH)

    def send(self, g, h, p, recv_sem, axis, step):
        self.copy(g, h, p, recv_sem, self.neighbour(g, axis, step)).start()

    def arrived(self, g, h, p, recv_sem):
        self.copy(g, h, p, recv_sem, self.neighbour(g, 0, 1)).wait_recv()

    def first(self, g):
        p = self.slot(g, 0, 0)
        for h in (0, 1):
            self.send(g, h, p, self.early(g, 3, h), 0, 1)
            self.send(g, h, p, self.early(g, 1, h), 0, 3)

    def second(self, g, n, da):
        p = self.slot(g, da, 0)
        for h in (0, 1):
            self.send(g, h, p, self.rest(n, h) if h else self.relayed(g, n, 0), 1, 1)
            self.send(g, h, p, self.relayed(g, n, 1) if h else self.rest(n, h), 1, 3)

    def relay(self, g):
        for d, h, step in ((3, 0, 1), (1, 1, 3)):
            p = self.slot(g, d, 0)
            self.arrived(g, h, p, self.early(g, d, h))
            self.send(g, h, p, self.early(g, 2, h), 0, step)

    def s1(self, g):
        for n, d, h in ((1, 3, 1), (2, 1, 0)):
            self.arrived(g, h, self.slot(g, d, 0), self.early(g, d, h))
            self.second(g, n, d)

    def s2(self, g):
        p = self.slot(g, 2, 0)
        for h in (0, 1):
            self.arrived(g, h, p, self.early(g, 2, h))
        self.second(g, 3, 2)

    def s3(self, g, n):
        d = around(n)
        for db, h, step in ((3, 0, 1), (1, 1, 3)):
            p = self.slot(g, d, db)
            self.arrived(g, h, p, self.relayed(g, n, h))
            self.send(g, h, p, self.rest(4, h), 1, step)

    def gathered(self, ref, sem):
        pltpu.make_async_copy(ref, ref, sem).wait()

    def finish(self):
        for h, ref in enumerate(self.sent):
            self.gathered(ref, self.send_sem.at[h])


def rotate(u, table):
    turned = pltpu.roll(table, 64, 1)
    first = lax.broadcasted_iota(jnp.int32, table.shape, 1) < 64
    cosine = jnp.where(first, table, turned)
    sine = jnp.where(first, -turned, table)
    return u * cosine + pltpu.roll(u, 64, 1) * sine


def kernel(tok_in, gain, cs, qw, kw, vw, out,
           tok, rq, rk, rv, tq, csq, wkv, wq, kb, vb, qt, acc, top, proj, sbuf, osend, obuf,
           tok_s, loc_s, zs, zr, ws, wr, ts, tr, fs, fr,
           s_a, r_a, x_a, s_b, r_b, x_b, s_c, r_c, x_c, s_d, r_d, x_d, os_, or_, outs_):
    c, f = lax.axis_index("ctx"), lax.axis_index("fsdp")
    zl, x, y = c // 16, lax.rem(c // 4, 4), lax.rem(c, 4)
    zh, k = f // 2, lax.rem(f, 2)
    col = x * 4 + y
    at = {"zl": zl, "x": x, "y": y, "f": f}
    head = zl * 2 + k

    def device(zh_, zl_, k_):
        return {"ctx": zl_ * 16 + col, "fsdp": zh_ * 2 + k_}

    def remote(src, dst, ss, rs, dev):
        return pltpu.make_async_remote_copy(src_ref=src, dst_ref=dst, send_sem=ss, recv_sem=rs, device_id=dev,
                                            device_id_type=pl.DeviceIdType.MESH)

    core = device(zh, zl, 1 - k)
    chip = device(zh, 1 - zl, k)
    diagonal = device(zh, 1 - zl, 1 - k)
    step_a = 1 + 2 * zl
    slab_a = lax.rem(zh + 4 - step_a, 4)
    slab_c = lax.rem(zh + step_a, 4)
    slab_b = lax.rem(zh + 2, 4)
    push_to = [(step_a, slab_a, zl_, k_) for zl_ in (0, 1) for k_ in (0, 1)] + [(2, slab_b, 1 - zl, k_) for k_ in (0, 1)]

    barrier = pltpu.get_barrier_semaphore()
    ring = PlaneGather(at, None, (None, None, None), None, None)
    friends = [device(slab_b, 1 - zl, k_) for k_ in (0, 1)]
    friends += [device(slab_a, zl_, k_) for zl_ in (0, 1) for k_ in (0, 1)]
    friends += [device(slab_c, zl, k_) for k_ in (0, 1)]
    friends += [core, chip, diagonal]
    friends += [ring.neighbour(0, axis, step) for axis in (0, 1) for step in (1, 3)]
    for friend in friends:
        pl.semaphore_signal(barrier, inc=1, device_id=friend, device_id_type=pl.DeviceIdType.MESH)

    rows = pl.ds(pl.multiple_of(col * 32, 32), 32)
    loads = [pltpu.make_async_copy(tok_in.at[pl.ds(i * 64, 64), :], tok.at[pl.ds(i * 64, 64), :], tok_s.at[i]) for i in (0, 1)]
    staged = [pltpu.make_async_copy(src.at[rows, :], dst, tok_s.at[2 + i])
              for i, (src, dst) in enumerate(((kw, rk), (vw, rv), (qw, rq)))]
    own = [
        pltpu.make_async_copy(kw.at[:, pl.ds(pl.multiple_of(head * 128, 128), 128)], wkv.at[k, :, pl.ds(0, 128)], loc_s.at[0]),
        pltpu.make_async_copy(vw.at[:, pl.ds(pl.multiple_of(head * 128, 128), 128)], wkv.at[k, :, pl.ds(128, 128)], loc_s.at[1]),
        pltpu.make_async_copy(qw.at[:, pl.ds(pl.multiple_of(head * 512, 512), 512)], wq.at[k], loc_s.at[2]),
    ]
    for copy in loads + staged + own:
        copy.start()

    def norm_rows(i, _):
        line = pl.ds(pl.multiple_of(i * 16, 16), 16)
        values = tok[line, :].astype(F32)
        inverse = lax.rsqrt(jnp.mean(values * values, axis=-1, keepdims=True) + EPS)
        tq[k, line, :] = (values * inverse * gain[...]).astype(BF16)
        return 0

    for i, copy in enumerate(loads):
        copy.wait()
        lax.fori_loop(i * 4, i * 4 + 4, norm_rows, 0)
    csq[k] = cs[...]
    for copy in staged:
        copy.wait()

    pl.semaphore_wait(barrier, len(friends))

    def pushes(n, what):
        r, slab, zl_, k_ = push_to[n]
        j = zl_ * 2 + k_
        index = r * 2 + k
        dev = device(slab, zl_, k_)
        narrow = pl.ds(pl.multiple_of(j * 128, 128), 128)
        wide = pl.ds(pl.multiple_of(j * 512, 512), 512)
        src, dst = (
            (rk.at[:, narrow], wkv.at[index, rows, pl.ds(0, 128)]),
            (rv.at[:, narrow], wkv.at[index, rows, pl.ds(128, 128)]),
            (rq.at[:, wide], wq.at[index, rows, :]),
        )[what]
        return remote(src, dst, zs.at[what // 2], zr.at[what // 2], dev)

    def whole(ref, sem):
        pltpu.make_async_copy(ref, ref, sem).wait()

    for n in (4, 5, 0, 1, 2, 3):
        pushes(n, 0).start()
        pushes(n, 1).start()
    for n in (4, 5, 0, 1, 2, 3):
        pushes(n, 2).start()

    other = zl * 2 + (1 - k)
    to_core = [
        remote(kw.at[:, pl.ds(pl.multiple_of(other * 128, 128), 128)], wkv.at[k, :, pl.ds(0, 128)], ws.at[0], wr.at[0], core),
        remote(vw.at[:, pl.ds(pl.multiple_of(other * 128, 128), 128)], wkv.at[k, :, pl.ds(128, 128)], ws.at[1], wr.at[1], core),
        remote(qw.at[:, pl.ds(pl.multiple_of(other * 512, 512), 512)], wq.at[k], ws.at[2], wr.at[2], core),
        remote(tq.at[k], tq.at[k], ws.at[3], wr.at[3], core),
        remote(cs, csq.at[k], ws.at[4], wr.at[4], core),
    ]
    for copy in to_core:
        copy.start()

    def quarter(q, i):
        return tq.at[q, :, pl.ds(i * 1024, 1024)]

    def to_chip(i):
        if i == 0:
            return remote(cs, csq.at[2 + k], ts.at[0], tr.at[0], chip)
        return remote(quarter(k, i - 1), quarter(2 + k, i - 1), ts.at[i], tr.at[i], chip)

    def from_chip(i):
        ref = csq.at[2 + k] if i == 0 else quarter(2 + k, i - 1)
        return remote(ref, ref, ts.at[i], tr.at[i], chip)

    def onward(i):
        ref = csq.at[2 + k] if i == 0 else quarter(2 + k, i - 1)
        return remote(ref, ref, fs.at[i], fr.at[i], core)

    def handed(i):
        ref = csq.at[3 - k] if i == 0 else quarter(3 - k, i - 1)
        return remote(ref, ref, fs.at[i], fr.at[i], core)

    for i in range(5):
        to_chip(i).start()

    def pass_on(*which):
        for i in which:
            from_chip(i).wait_recv()
            onward(i).start()

    def pieces(w):
        return lambda g, h, p: w.at[pl.ds(2 + 3 * g, 3), pl.ds(pl.multiple_of(p * 32 + 16 * h, 16), 16), :]

    wkv_g = PlaneGather(at, pieces(wkv), (s_a, r_a, x_a), lambda n, h: 0, (wkv.at[0:6, 0:480],))
    wq_g = PlaneGather(at, pieces(wq), (s_b, r_b, x_b), lambda n, h: 0, (wq.at[0:6, 0:480],))
    kv_g = [PlaneGather(at, lambda g, h, p, m=m: vb.at[g, p, m] if h else kb.at[g, p, m], sems, lambda n, h: n * 2 + h,
                        (kb.at[:, 0:15, 0], vb.at[:, 0:15, 0]))
            for m, sems in enumerate(((s_c, r_c, x_c), (s_d, r_d, x_d)))]

    def kv_third(m, n):
        whole(kb.at[:, 0, 0], kv_g[m].rest(n, 0))
        whole(vb.at[:, 0, 0], kv_g[m].rest(n, 1))

    def kv_fourth(m):
        whole(kb.at[:, 0:4, 0], kv_g[m].rest(4, 0))
        whole(vb.at[:, 0:4, 0], kv_g[m].rest(4, 1))

    def both(step):
        for g in (0, 1):
            step(g)

    def each(step, lo, hi):
        def body(n, _):
            for g in (0, 1):
                step(g, n)
            return 0

        lax.fori_loop(lo, hi, body, 0)

    def third(gather, n):
        for g in (0, 1):
            gather.s3(g, n)

    def sideways(gather):
        for g in (0, 1):
            gather.second(g, 0, 0)

    def features(lo, count, r):
        start = pl.multiple_of(lax.rem(zh + r, 4) * 1024, 1024)
        return tq[lo:lo + count, :, pl.ds(start, 1024)].reshape(count * 128, 1024)

    lane = lax.broadcasted_iota(jnp.int32, (1, 128), 1)
    offset = lax.rem(lane, 64).astype(F32)

    def accumulate(r, lo, count, w, width):
        part = jnp.dot(features(lo, count, r), w, preferred_element_type=F32)
        size = count * 128

        @pl.when(r == 0)
        def _():
            proj[0:size, 0:width] = part

        @pl.when(r > 0)
        def _():
            proj[0:size, 0:width] = proj[0:size, 0:width] + part

    def make_kv(m):
        def project(r, _):
            accumulate(r, 2 * m, 2, wkv[pl.ds(2 * r, 2)].reshape(1024, 256), 256)
            return 0

        lax.fori_loop(0, 4, project, 0)
        for g in (0, 1):
            i = m * 2 + g
            key = rotate(proj[g * 128:g * 128 + 128, 0:128], csq[i, 0:128, :])
            kb[g, col, m, 0:128, :] = key.astype(BF16)
            vb[g, col, m] = proj[g * 128:g * 128 + 128, 128:256].T.astype(BF16)
            block = (csq[i, 128:129, :] - offset) * (1.0 / 64.0)
            kb[g, col, m, 128:144, :] = jnp.broadcast_to(block, (16, 128)).astype(BF16)

    def project_q(r, _):
        accumulate(r, 0, 4, wq[pl.ds(2 * r, 2)].reshape(1024, 512), 512)
        return 0

    whole(wkv.at[2:8, 0:32], zr.at[0])
    kv_a, kv_b = kv_g
    both(wkv_g.first)
    sideways(wkv_g)
    both(wkv_g.relay)
    both(wkv_g.s1)
    whole(wq.at[2:8, 0:32], zr.at[1])
    both(wq_g.first)
    both(wkv_g.s2)
    sideways(wq_g)
    third(wkv_g, 0)
    both(wq_g.relay)
    third(wkv_g, 1)
    third(wkv_g, 3)
    third(wkv_g, 2)
    both(wq_g.s1)
    whole(wkv.at[0:6, 0:256], x_a.at[0])
    both(wq_g.s2)
    own[0].wait()
    own[1].wait()
    for i in (0, 1, 3, 4):
        to_core[i].wait_recv()
    make_kv(0)
    both(kv_a.first)
    pass_on(0, 1, 2, 3)
    each(wq_g.s3, 0, 3)
    both(kv_a.relay)
    both(kv_a.s1)
    third(wq_g, 3)
    pass_on(4)
    for i in range(5):
        handed(i).wait_recv()
    make_kv(1)
    third(kv_a, 1)
    both(kv_b.first)
    both(kv_a.s2)
    sideways(kv_a)
    whole(wq.at[0:6, 0:256], x_b.at[0])
    own[2].wait()
    to_core[2].wait_recv()
    lax.fori_loop(0, 2, project_q, 0)
    third(kv_a, 2)
    both(kv_b.relay)
    third(kv_a, 3)
    both(kv_b.s1)
    third(kv_a, 0)
    lax.fori_loop(2, 4, project_q, 0)
    sideways(kv_b)

    edge = lax.broadcasted_iota(jnp.int32, (128, 128), 0)
    for i in range(4):
        block = (csq[i, 128:129, :] - offset) * (1.0 / 64.0)
        later = jnp.where(edge.astype(F32) > block, FLOOR, 0.0).astype(BF16)
        for hd in range(GROUP):
            u = rotate(proj[pl.ds(i * 128, 128), pl.ds(hd * 128, 128)], csq[i, 0:128, :])
            at_col = ((i // 2) * GROUP + hd) * 128
            qt[i % 2, 0:128, at_col:at_col + 128] = u.T.astype(BF16)
            qt[i % 2, 128:256, at_col:at_col + 128] = later
    acc[...] = jnp.zeros_like(acc)
    top[...] = jnp.full_like(top, FLOOR)
    both(kv_b.s2)

    scale = HEAD ** -0.5 * LOG2E
    upper = edge < 64
    across = lax.broadcasted_iota(jnp.int32, (128, 128), 1)
    triangle = jnp.where((edge > across) & ((edge < 64) == (across < 64)), FLOOR, 0.0)
    numbers = across.astype(F32)
    ones = jnp.ones((16, 512), BF16)

    def attend(i, halves):
        m, turn = i // 4, lax.rem(i, 4)
        ends = (turn == 0) | (turn == 3)
        slots = []
        for e in range(4):
            da = around(jnp.where(ends, e, 2 * (turn - 1) + e // 2))
            db = jnp.where(turn == 0, 0, jnp.where(turn == 3, 2, 3 - 2 * (e % 2)))
            slots.append((da, db))
        work = []
        for g in (0, 1):
            keys, values, runs = [], [], []
            for da, db in slots:
                p = kv_g[0].slot(g, da, db)
                keys.append(kb[g, p, m, 0:128, :])
                values.append(vb[g, p, m])
                block = kb[g, p, m, 128:144, :].astype(F32)[0:1, :]
                run = jnp.where(upper, block[:, 0:1], block[:, 64:65])
                runs.append(jnp.where(run == numbers, 1.0, 0.0).astype(BF16))
            keys = jnp.concatenate([jnp.concatenate(keys, axis=0), jnp.concatenate(runs, axis=0)], axis=1)
            values = jnp.concatenate([jnp.concatenate(values, axis=1), ones], axis=0)
            for half in halves:
                own_run = triangle * jnp.where((turn == 0) & (m == half), 1.0, 0.0)
                for tile in (0, 1):
                    work.append((g, keys, values, own_run, pl.ds(pl.multiple_of(half * 512 + tile * 256, 256), 256)))

        def score(t):
            g, keys, _, own_run, cols = work[t]
            scores = jnp.dot(keys, qt[g, :, cols], preferred_element_type=F32)
            first = scores[0:128] + jnp.concatenate([own_run, own_run], axis=1)
            sbuf[t % 2, 0:128] = first
            sbuf[t % 2, 128:512] = scores[128:512]
            return jnp.maximum(jnp.max(first, axis=0, keepdims=True), jnp.max(scores[128:512], axis=0, keepdims=True))

        best = score(0)
        for t in range(len(work)):
            g, _, values, _, cols = work[t]
            following = score(t + 1) if t + 1 < len(work) else None
            before = top[g, 0:1, cols]
            now = jnp.maximum(before, best)
            probs = jnp.exp2((sbuf[t % 2] - now) * scale).astype(BF16)
            factor = jnp.exp2((before - now) * scale)
            acc[g, :, cols] = acc[g, :, cols] * factor + jnp.dot(values, probs, preferred_element_type=F32)
            top[g, 0:1, cols] = now
            best = following

    def settle(m):
        for g in (0, 1):
            for hd in range(GROUP):
                at_col = m * 512 + hd * 128
                one = acc[g, 0:128, at_col:at_col + 128] / acc[g, 128:129, at_col:at_col + 128]
                osend[m * 2 + g, :, hd * 128:hd * 128 + 128] = one.T.astype(BF16)

    def give(n):
        src, dev = ((2 + k, chip), (3 - k, diagonal), (1 - k, core))[n]
        return remote(osend.at[src], obuf.at[head], os_.at[n], or_.at[n], dev)

    def take(n):
        j = ((1 - zl) * 2 + k, (1 - zl) * 2 + 1 - k, zl * 2 + 1 - k)[n]
        return j, remote(obuf.at[j], obuf.at[j], os_.at[n], or_.at[n], core)

    def round_both(i, _):
        @pl.when(i == 1)
        def _():
            third(kv_b, 1)
            kv_third(0, 0)
            kv_third(0, 1)

        @pl.when(i == 2)
        def _():
            third(kv_b, 2)
            kv_third(0, 2)
            kv_third(0, 3)

        @pl.when(i == 3)
        def _():
            kv_fourth(0)
            third(kv_b, 0)

        attend(i, (1, 0))
        return 0

    def round_one(step, _):
        @pl.when(step == 0)
        def _():
            third(kv_b, 3)

        @pl.when(step == 1)
        def _():
            kv_third(1, 0)
            kv_third(1, 1)

        @pl.when(step == 2)
        def _():
            kv_third(1, 2)
            kv_third(1, 3)

        @pl.when(step == 3)
        def _():
            kv_fourth(1)

        @pl.when(step == 4)
        def _():
            settle(1)
            give(0).start()
            give(1).start()

        attend(4 + lax.rem(step, 4), (jnp.where(step < 4, 1, 0),))
        return 0

    lax.fori_loop(0, 4, round_both, 0)
    lax.fori_loop(0, 8, round_one, 0)
    settle(0)
    give(2).start()

    def store(src, j, n):
        return pltpu.make_async_copy(src, out.at[:, pl.ds(pl.multiple_of(j * 512, 512), 512)], outs_.at[n])

    last = [store(osend.at[k], head, 3)]
    last[0].start()
    whole(wkv.at[2:8, 0:32], zs.at[0])
    whole(wq.at[2:8, 0:32], zs.at[1])
    for copy in to_core:
        copy.wait_send()
    for i in range(5):
        to_chip(i).wait_send()
        onward(i).wait_send()
    for gather in (wkv_g, wq_g, kv_g[0], kv_g[1]):
        gather.finish()
    for n in (2, 0, 1):
        j, arrival = take(n)
        arrival.wait_recv()
        last.append(store(obuf.at[j], j, n))
        last[-1].start()
    for n in range(3):
        give(n).wait_send()
    for copy in last:
        copy.wait()


def on_device(tokens, positions, norm_gain, query_weight, key_weight, value_matrix):
    places = positions[0]
    table = jnp.concatenate([rope_tables(places), jnp.broadcast_to(places.astype(F32)[None, :], (8, 128))], axis=0)
    vmem = pl.BlockSpec(memory_space=pltpu.VMEM)
    anywhere = pl.BlockSpec(memory_space=pl.ANY)
    far = pl.BlockSpec(memory_space=pltpu.HBM)
    dma = pltpu.SemaphoreType.DMA
    result = pl.pallas_call(
        kernel,
        out_shape=jax.ShapeDtypeStruct((128, 2048), BF16),
        in_specs=[far, vmem, vmem, far, far, far],
        out_specs=anywhere,
        scratch_shapes=[
            pltpu.VMEM((128, 4096), BF16),
            pltpu.VMEM((32, 2048), BF16),
            pltpu.VMEM((32, 512), BF16),
            pltpu.VMEM((32, 512), BF16),
            pltpu.VMEM((4, 128, 4096), BF16),
            pltpu.VMEM((4, 136, 128), F32),
            pltpu.VMEM((8, 512, 256), BF16),
            pltpu.VMEM((8, 512, 512), BF16),
            pltpu.VMEM((2, 16, 2, 144, 128), BF16),
            pltpu.VMEM((2, 16, 2, 128, 128), BF16),
            pltpu.VMEM((2, 256, 1024), BF16),
            pltpu.VMEM((2, 144, 1024), F32),
            pltpu.VMEM((2, 8, 1024), F32),
            pltpu.VMEM((512, 512), F32),
            pltpu.VMEM((2, 512, 256), F32),
            pltpu.VMEM((4, 128, 512), BF16),
            pltpu.VMEM((4, 128, 512), BF16),
            dma((5,)), dma((3,)), dma((2,)), dma((2,)), dma((5,)), dma((5,)), dma((5,)), dma((5,)), dma((5,)), dma((5,)),
            dma((1,)), dma((2, 14)), dma((1,)), dma((1,)), dma((2, 14)), dma((1,)),
            dma((2,)), dma((2, 14)), dma((10,)), dma((2,)), dma((2, 14)), dma((10,)),
            dma((3,)), dma((3,)), dma((4,)),
        ],
        compiler_params=pltpu.CompilerParams(
            collective_id=0, has_side_effects=True, vmem_limit_bytes=53 * 1024 * 1024),
    )(tokens[0], norm_gain[None, :], table, query_weight, key_weight, value_matrix)
    return result[None]


def solution(mesh):
    placed = (
        P("fsdp", "ctx", None),
        P("fsdp", "ctx"),
        P(),
        P("fsdp", None),
        P("fsdp", None),
        P("fsdp", None),
    )
    return jax.shard_map(
        on_device, mesh=mesh, in_specs=placed, out_specs=P("fsdp", "ctx", None), check_vma=False
    )
```

time: 104 us -> 79.4 us (0.76)
  Pallas kernels: 100 us -> 76.6 us
    pallas_call x1, Pallas kernels: 100 us -> 76.6 us  [on_device(): pl.pallas_call(kernel, out_shape=jax.ShapeDtypeStruct((128, 2048), BF16),...]
where the time goes in v2:
time: 79.4 us; the launch traced here: 79.2 us
  Pallas kernels  76.6 us (96%)
  local copies, waits for them, and re-layouts  1.51 us (2%)
  other arithmetic  1.06 us (1%)
    pallas_call x1, Pallas kernels, on_device(): pl.pallas_call(kernel, out_shape=jax.ShapeDtypeStruct((128, 2048), BF16),...  76.6 us

profile of v2, /device:TPU:1, one launch (start us, length us, event | category | flops | bytes accessed | tf_op | source)
XLA Modules:
  0.0 79.2 jit_solution(17685018859828082189)
XLA Ops:
  0.0 0.7 convert_bitcast_fusion
  0.7 0.3 multiply_cosine_fusion
  1.0 0.1 pad_maximum_fusion.cs
  1.1 0.0 copy-start
  1.1 0.7 copy-done
  1.8 76.6 %shard_map.64 = bf16[128,2048]{1,0:T(8,128)(2,1)S(1)} custom-call(bf16[128,4096]{1,0:T(8,128)(2,1)} %bitcast.7, f32[1,4096]{1,0:T(1,128)S(1)} %bitcast.6, f32[136,128]{1,0:T(8,128)S(1)} %pad_maximum_fusion.cs, bf16[512,2048]{1,0:T(8,128)(2,1)} %qw.1, bf16[512,512]{1,0:T(8,128)(2,1)} %kw.1, bf16[512,512]{1,0:T(8,128)(2,1)} %vw.1), custom_call_target="tpu_custom_call" | custom-call | tf_op jit(solution)/shard_map/pallas_call | solution.py:534
  78.4 0.8 %copy.8 = bf16[1,128,2048]{2,1,0:T(8,128)(2,1)} copy(bf16[1,128,2048]{2,1,0:T(8,128)(2,1)S(1)} %bitcast.5) | data formatting | bytes 1048576
  (2 shorter events, 0.0 us)
Async XLA Ops:
  1.1 0.7 copy-start

commit v3 on v2

--- a/solution.py
+++ b/solution.py
@@ -16,13 +16,6 @@
 F32, BF16 = jnp.float32, jnp.bfloat16
 
 
-def rope_tables(places):
-    half = HEAD // 2
-    frequency = BASE ** (-(jnp.arange(half, dtype=F32) * 2.0) / HEAD)
-    angles = places.astype(F32)[:, None] * frequency[None, :]
-    return jnp.concatenate([jnp.cos(angles), jnp.sin(angles)], axis=1)
-
-
 def around(n):
     return jnp.where(n == 0, 0, jnp.where(n == 1, 3, jnp.where(n == 2, 1, 2)))
 
@@ -33,7 +26,10 @@
         self.send_sem, self.recv_sem, self.rest_sem, self.shared = *sems, shared
 
     def slot(self, g, da, db):
-        dx, dy = (da, db) if g == 0 else (db, da)
+        if isinstance(g, int):
+            dx, dy = (da, db) if g == 0 else (db, da)
+        else:
+            dx, dy = jnp.where(g == 0, da, db), jnp.where(g == 0, db, da)
         return lax.rem(self.at["x"] + dx, 4) * 4 + lax.rem(self.at["y"] + dy, 4)
 
     def neighbour(self, g, axis, step):
@@ -115,7 +111,7 @@
     return u * cosine + pltpu.roll(u, 64, 1) * sine
 
 
-def kernel(tok_in, gain, cs, qw, kw, vw, out,
+def kernel(tok_in, table, qw, kw, vw, out,
            tok, rq, rk, rv, tq, csq, wkv, wq, kb, vb, qt, acc, top, proj, sbuf, osend, obuf,
            tok_s, loc_s, zs, zr, ws, wr, ts, tr, fs, fr,
            s_a, r_a, x_a, s_b, r_b, x_b, s_c, r_c, x_c, s_d, r_d, x_d, os_, or_, outs_):
@@ -140,7 +136,7 @@
     slab_a = lax.rem(zh + 4 - step_a, 4)
     slab_c = lax.rem(zh + step_a, 4)
     slab_b = lax.rem(zh + 2, 4)
-    push_to = [(step_a, slab_a, zl_, k_) for zl_ in (0, 1) for k_ in (0, 1)] + [(2, slab_b, 1 - zl, k_) for k_ in (0, 1)]
+    push_to = [(step_a, slab_a, zl_, k_) for zl_ in (1 - zl, zl) for k_ in (0, 1)] + [(2, slab_b, 1 - zl, k_) for k_ in (0, 1)]
 
     barrier = pltpu.get_barrier_semaphore()
     ring = PlaneGather(at, None, (None, None, None), None, None)
@@ -168,13 +164,9 @@
         line = pl.ds(pl.multiple_of(i * 16, 16), 16)
         values = tok[line, :].astype(F32)
         inverse = lax.rsqrt(jnp.mean(values * values, axis=-1, keepdims=True) + EPS)
-        tq[k, line, :] = (values * inverse * gain[...]).astype(BF16)
+        tq[k, line, :] = (values * inverse * table[:, 0:4096]).astype(BF16)
         return 0
 
-    for i, copy in enumerate(loads):
-        copy.wait()
-        lax.fori_loop(i * 4, i * 4 + 4, norm_rows, 0)
-    csq[k] = cs[...]
     for copy in staged:
         copy.wait()
 
@@ -192,6 +184,9 @@
             (rv.at[:, narrow], wkv.at[index, rows, pl.ds(128, 128)]),
             (rq.at[:, wide], wq.at[index, rows, :]),
         )[what]
+        if what == 2 and n < 2:
+            src, dst = qw.at[:, wide], wq.at[index]
+            return remote(src, dst, zs.at[2], zr.at[2], dev)
         return remote(src, dst, zs.at[what // 2], zr.at[what // 2], dev)
 
     def whole(ref, sem):
@@ -200,8 +195,19 @@
     for n in (4, 5, 0, 1, 2, 3):
         pushes(n, 0).start()
         pushes(n, 1).start()
-    for n in (4, 5, 0, 1, 2, 3):
+    for n in (4, 5, 2, 3):
         pushes(n, 2).start()
+
+    for i, copy in enumerate(loads):
+        copy.wait()
+        lax.fori_loop(i * 4, i * 4 + 4, norm_rows, 0)
+    step_in = lax.broadcasted_iota(jnp.int32, (128, 128), 0)
+    place = table[:, 4096:4224]
+    column = jnp.where(step_in < 64, place[:, 0:1], place[:, 64:65]) + lax.rem(step_in, 64).astype(F32)
+    angles = column * table[:, 4224:4352]
+    first_half = lax.broadcasted_iota(jnp.int32, (128, 128), 1) < 64
+    csq[k, 0:128, :] = jnp.where(first_half, jnp.cos(angles), jnp.sin(angles))
+    csq[k, 128:136, :] = jnp.broadcast_to(place, (8, 128))
 
     other = zl * 2 + (1 - k)
     to_core = [
@@ -209,7 +215,7 @@
         remote(vw.at[:, pl.ds(pl.multiple_of(other * 128, 128), 128)], wkv.at[k, :, pl.ds(128, 128)], ws.at[1], wr.at[1], core),
         remote(qw.at[:, pl.ds(pl.multiple_of(other * 512, 512), 512)], wq.at[k], ws.at[2], wr.at[2], core),
         remote(tq.at[k], tq.at[k], ws.at[3], wr.at[3], core),
-        remote(cs, csq.at[k], ws.at[4], wr.at[4], core),
+        remote(csq.at[k], csq.at[k], ws.at[4], wr.at[4], core),
     ]
     for copy in to_core:
         copy.start()
@@ -219,7 +225,7 @@
 
     def to_chip(i):
         if i == 0:
-            return remote(cs, csq.at[2 + k], ts.at[0], tr.at[0], chip)
+            return remote(csq.at[k], csq.at[2 + k], ts.at[0], tr.at[0], chip)
         return remote(quarter(k, i - 1), quarter(2 + k, i - 1), ts.at[i], tr.at[i], chip)
 
     def from_chip(i):
@@ -242,11 +248,14 @@
             from_chip(i).wait_recv()
             onward(i).start()
 
-    def pieces(w):
-        return lambda g, h, p: w.at[pl.ds(2 + 3 * g, 3), pl.ds(pl.multiple_of(p * 32 + 16 * h, 16), 16), :]
-
-    wkv_g = PlaneGather(at, pieces(wkv), (s_a, r_a, x_a), lambda n, h: 0, (wkv.at[0:6, 0:480],))
-    wq_g = PlaneGather(at, pieces(wq), (s_b, r_b, x_b), lambda n, h: 0, (wq.at[0:6, 0:480],))
+    def part(g, h, p):
+        return wkv.at[pl.ds(2 + 3 * g, 3), pl.ds(pl.multiple_of(p * 32 + 16 * h, 16), 16), :]
+
+    def part_q(g, h, p):
+        return wq.at[pl.ds(2 + 2 * zl + 2 * g, 2), pl.ds(pl.multiple_of(p * 32 + 16 * h, 16), 16), :]
+
+    wkv_g = PlaneGather(at, part, (s_a, r_a, x_a), lambda n, h: 0, (wkv.at[0:6, 0:480],))
+    wq_g = PlaneGather(at, part_q, (s_b, r_b, x_b), lambda n, h: 0, (wq.at[0:4, 0:480],))
     kv_g = [PlaneGather(at, lambda g, h, p, m=m: vb.at[g, p, m] if h else kb.at[g, p, m], sems, lambda n, h: n * 2 + h,
                         (kb.at[:, 0:15, 0], vb.at[:, 0:15, 0]))
             for m, sems in enumerate(((s_c, r_c, x_c), (s_d, r_d, x_d)))]
@@ -312,71 +321,81 @@
             block = (csq[i, 128:129, :] - offset) * (1.0 / 64.0)
             kb[g, col, m, 128:144, :] = jnp.broadcast_to(block, (16, 128)).astype(BF16)
 
-    def project_q(r, _):
+    def project_q(q, _):
+        near = 3 - 2 * zl
+        r = jnp.where(q == 0, 0, jnp.where(q == 1, near, jnp.where(q == 2, 2, 4 - near)))
         accumulate(r, 0, 4, wq[pl.ds(2 * r, 2)].reshape(1024, 512), 512)
         return 0
 
     whole(wkv.at[2:8, 0:32], zr.at[0])
     kv_a, kv_b = kv_g
+    edge = lax.broadcasted_iota(jnp.int32, (128, 128), 0)
+    for n in (0, 1):
+        pushes(n, 2).start()
     both(wkv_g.first)
     sideways(wkv_g)
+    acc[...] = jnp.zeros_like(acc)
+    top[...] = jnp.full_like(top, FLOOR)
     both(wkv_g.relay)
     both(wkv_g.s1)
-    whole(wq.at[2:8, 0:32], zr.at[1])
+    whole(wq.at[2:6, 0:32], zr.at[1])
     both(wq_g.first)
     both(wkv_g.s2)
+    third(wkv_g, 0)
     sideways(wq_g)
-    third(wkv_g, 0)
-    both(wq_g.relay)
+    third(wkv_g, 2)
+    pass_on(0)
     third(wkv_g, 1)
     third(wkv_g, 3)
-    third(wkv_g, 2)
+    both(wq_g.relay)
     both(wq_g.s1)
+    pass_on(1)
+    third(wq_g, 0)
+    both(wq_g.s2)
     whole(wkv.at[0:6, 0:256], x_a.at[0])
-    both(wq_g.s2)
     own[0].wait()
     own[1].wait()
     for i in (0, 1, 3, 4):
         to_core[i].wait_recv()
     make_kv(0)
     both(kv_a.first)
-    pass_on(0, 1, 2, 3)
-    each(wq_g.s3, 0, 3)
+    sideways(kv_a)
+    third(wq_g, 2)
+    pass_on(2)
+    third(wq_g, 3)
+    third(wq_g, 1)
     both(kv_a.relay)
+    pass_on(3, 4)
     both(kv_a.s1)
-    third(wq_g, 3)
-    pass_on(4)
     for i in range(5):
         handed(i).wait_recv()
     make_kv(1)
-    third(kv_a, 1)
     both(kv_b.first)
     both(kv_a.s2)
-    sideways(kv_a)
-    whole(wq.at[0:6, 0:256], x_b.at[0])
+    sideways(kv_b)
     own[2].wait()
     to_core[2].wait_recv()
-    lax.fori_loop(0, 2, project_q, 0)
-    third(kv_a, 2)
-    both(kv_b.relay)
-    third(kv_a, 3)
-    both(kv_b.s1)
-    third(kv_a, 0)
-    lax.fori_loop(2, 4, project_q, 0)
-    sideways(kv_b)
-
-    edge = lax.broadcasted_iota(jnp.int32, (128, 128), 0)
     for i in range(4):
         block = (csq[i, 128:129, :] - offset) * (1.0 / 64.0)
         later = jnp.where(edge.astype(F32) > block, FLOOR, 0.0).astype(BF16)
         for hd in range(GROUP):
+            at_col = ((i // 2) * GROUP + hd) * 128
+            qt[i % 2, 128:256, at_col:at_col + 128] = later
+    lax.fori_loop(0, 1, project_q, 0)
+    whole(wq.at[0:2], zr.at[2])
+    lax.fori_loop(1, 2, project_q, 0)
+    third(kv_a, 0)
+    third(kv_a, 1)
+    whole(wq.at[0:4, 0:256], x_b.at[0])
+    lax.fori_loop(2, 4, project_q, 0)
+    for i in range(4):
+        for hd in range(GROUP):
             u = rotate(proj[pl.ds(i * 128, 128), pl.ds(hd * 128, 128)], csq[i, 0:128, :])
             at_col = ((i // 2) * GROUP + hd) * 128
             qt[i % 2, 0:128, at_col:at_col + 128] = u.T.astype(BF16)
-            qt[i % 2, 128:256, at_col:at_col + 128] = later
-    acc[...] = jnp.zeros_like(acc)
-    top[...] = jnp.full_like(top, FLOOR)
-    both(kv_b.s2)
+    both(kv_b.relay)
+    third(kv_a, 2)
+    third(kv_a, 3)
 
     scale = HEAD ** -0.5 * LOG2E
     upper = edge < 64
@@ -385,7 +404,7 @@
     numbers = across.astype(F32)
     ones = jnp.ones((16, 512), BF16)
 
-    def attend(i, halves):
+    def attend(i, halves, groups=(0, 1)):
         m, turn = i // 4, lax.rem(i, 4)
         ends = (turn == 0) | (turn == 3)
         slots = []
@@ -394,7 +413,7 @@
             db = jnp.where(turn == 0, 0, jnp.where(turn == 3, 2, 3 - 2 * (e % 2)))
             slots.append((da, db))
         work = []
-        for g in (0, 1):
+        for g in groups:
             keys, values, runs = [], [], []
             for da, db in slots:
                 p = kv_g[0].slot(g, da, db)
@@ -430,16 +449,18 @@
             top[g, 0:1, cols] = now
             best = following
 
-    def settle(m):
-        for g in (0, 1):
-            for hd in range(GROUP):
-                at_col = m * 512 + hd * 128
-                one = acc[g, 0:128, at_col:at_col + 128] / acc[g, 128:129, at_col:at_col + 128]
-                osend[m * 2 + g, :, hd * 128:hd * 128 + 128] = one.T.astype(BF16)
-
-    def give(n):
-        src, dev = ((2 + k, chip), (3 - k, diagonal), (1 - k, core))[n]
-        return remote(osend.at[src], obuf.at[head], os_.at[n], or_.at[n], dev)
+    def settle(m, g):
+        for hd in range(GROUP):
+            at_col = m * 512 + hd * 128
+            one = acc[g, 0:128, at_col:at_col + 128] / acc[g, 128:129, at_col:at_col + 128]
+            osend[m * 2 + g, :, hd * 128:hd * 128 + 128] = one.T.astype(BF16)
+
+    def give_far(g):
+        n = lax.rem(g + k, 2)
+        return remote(osend.at[2 + g], obuf.at[head], os_.at[n], or_.at[n], device(zh, 1 - zl, g))
+
+    def give_near():
+        return remote(osend.at[1 - k], obuf.at[head], os_.at[2], or_.at[2], core)
 
     def take(n):
         j = ((1 - zl) * 2 + k, (1 - zl) * 2 + 1 - k, zl * 2 + 1 - k)[n]
@@ -448,20 +469,21 @@
     def round_both(i, _):
         @pl.when(i == 1)
         def _():
-            third(kv_b, 1)
+            both(kv_b.s1)
             kv_third(0, 0)
             kv_third(0, 1)
 
         @pl.when(i == 2)
         def _():
-            third(kv_b, 2)
+            both(kv_b.s2)
             kv_third(0, 2)
             kv_third(0, 3)
 
         @pl.when(i == 3)
         def _():
+            third(kv_b, 1)
+            third(kv_b, 0)
             kv_fourth(0)
-            third(kv_b, 0)
 
         attend(i, (1, 0))
         return 0
@@ -469,6 +491,7 @@
     def round_one(step, _):
         @pl.when(step == 0)
         def _():
+            third(kv_b, 2)
             third(kv_b, 3)
 
         @pl.when(step == 1)
@@ -481,23 +504,27 @@
             kv_third(1, 2)
             kv_third(1, 3)
 
-        @pl.when(step == 3)
-        def _():
-            kv_fourth(1)
-
-        @pl.when(step == 4)
-        def _():
-            settle(1)
-            give(0).start()
-            give(1).start()
-
-        attend(4 + lax.rem(step, 4), (jnp.where(step < 4, 1, 0),))
+        attend(4 + step, (1,))
         return 0
 
+    def last_round(g, _):
+        attend(7, (1,), (g,))
+        settle(1, g)
+        give_far(g).start()
+        return 0
+
+    def own_round(i, _):
+        attend(i, (0,))
+        return 0
+
     lax.fori_loop(0, 4, round_both, 0)
-    lax.fori_loop(0, 8, round_one, 0)
-    settle(0)
-    give(2).start()
+    lax.fori_loop(0, 3, round_one, 0)
+    kv_fourth(1)
+    lax.fori_loop(0, 2, last_round, 0)
+    lax.fori_loop(4, 8, own_round, 0)
+    settle(0, 0)
+    settle(0, 1)
+    give_near().start()
 
     def store(src, j, n):
         return pltpu.make_async_copy(src, out.at[:, pl.ds(pl.multiple_of(j * 512, 512), 512)], outs_.at[n])
@@ -505,7 +532,8 @@
     last = [store(osend.at[k], head, 3)]
     last[0].start()
     whole(wkv.at[2:8, 0:32], zs.at[0])
-    whole(wq.at[2:8, 0:32], zs.at[1])
+    whole(wq.at[2:6, 0:32], zs.at[1])
+    whole(wq.at[0:2], zs.at[2])
     for copy in to_core:
         copy.wait_send()
     for i in range(5):
@@ -518,15 +546,16 @@
         arrival.wait_recv()
         last.append(store(obuf.at[j], j, n))
         last[-1].start()
-    for n in range(3):
-        give(n).wait_send()
+    give_far(0).wait_send()
+    give_far(1).wait_send()
+    give_near().wait_send()
     for copy in last:
         copy.wait()
 
 
 def on_device(tokens, positions, norm_gain, query_weight, key_weight, value_matrix):
-    places = positions[0]
-    table = jnp.concatenate([rope_tables(places), jnp.broadcast_to(places.astype(F32)[None, :], (8, 128))], axis=0)
+    frequency = BASE ** (-(jnp.arange(HEAD // 2, dtype=F32) * 2.0) / HEAD)
+    table = jnp.concatenate([norm_gain, positions[0].astype(F32), frequency, frequency])[None, :]
     vmem = pl.BlockSpec(memory_space=pltpu.VMEM)
     anywhere = pl.BlockSpec(memory_space=pl.ANY)
     far = pl.BlockSpec(memory_space=pltpu.HBM)
@@ -534,7 +563,7 @@
     result = pl.pallas_call(
         kernel,
         out_shape=jax.ShapeDtypeStruct((128, 2048), BF16),
-        in_specs=[far, vmem, vmem, far, far, far],
+        in_specs=[far, vmem, far, far, far],
         out_specs=anywhere,
         scratch_shapes=[
             pltpu.VMEM((128, 4096), BF16),
@@ -554,14 +583,14 @@
             pltpu.VMEM((2, 512, 256), F32),
             pltpu.VMEM((4, 128, 512), BF16),
             pltpu.VMEM((4, 128, 512), BF16),
-            dma((5,)), dma((3,)), dma((2,)), dma((2,)), dma((5,)), dma((5,)), dma((5,)), dma((5,)), dma((5,)), dma((5,)),
+            dma((5,)), dma((3,)), dma((3,)), dma((3,)), dma((5,)), dma((5,)), dma((5,)), dma((5,)), dma((5,)), dma((5,)),
             dma((1,)), dma((2, 14)), dma((1,)), dma((1,)), dma((2, 14)), dma((1,)),
             dma((2,)), dma((2, 14)), dma((10,)), dma((2,)), dma((2, 14)), dma((10,)),
             dma((3,)), dma((3,)), dma((4,)),
         ],
         compiler_params=pltpu.CompilerParams(
             collective_id=0, has_side_effects=True, vmem_limit_bytes=53 * 1024 * 1024),
-    )(tokens[0], norm_gain[None, :], table, query_weight, key_weight, value_matrix)
+    )(tokens[0], table, query_weight, key_weight, value_matrix)
     return result[None]
 
 

time: 79.4 us -> 74.5 us (0.938)
  Pallas kernels: 76.6 us -> 72 us
    pallas_call x1, Pallas kernels: 76.6 us -> 72 us  [on_device(): pl.pallas_call(kernel, out_shape=jax.ShapeDtypeStruct((128, 2048), BF16),...]
    concatenate x0 -> x1, local copies, waits for them, and re-layouts: none -> 0.8 us  [on_device(): jnp.concatenate([norm_gain, positions[0].astype(F32), frequency, frequency])]
where the time goes in v3:
time: 74.5 us; the launch traced here: 74.3 us
  Pallas kernels  72 us (97%)
  local copies, waits for them, and re-layouts  1.6 us (2%)
    pallas_call x1, Pallas kernels, on_device(): pl.pallas_call(kernel, out_shape=jax.ShapeDtypeStruct((128, 2048), BF16),...  72 us

profile of v3, /device:TPU:1, one launch (start us, length us, event | category | flops | bytes accessed | tf_op | source)
XLA Modules:
  0.0 74.3 jit_solution(14260628345664638820)
XLA Ops:
  0.0 0.7 convert_bitcast_fusion
  0.7 0.8 %concatenate.3 = f32[4352]{0:T(1024)S(1)} concatenate(f32[4096]{0:T(1024)} %param.8, f32[128]{0:T(128)S(1)} %convert_bitcast_fusion, f32[64]{0:T(128)S(1)} %multiply_power_fusion, f32[64]{0:T(128)S(1)} %multiply_power_fusion), dimensions={0} | concatenate | bytes 34816 | tf_op jit(solution)/shard_map/concatenate | solution.py:558
  1.5 72.0 %shard_map.64 = bf16[128,2048]{1,0:T(8,128)(2,1)S(1)} custom-call(bf16[128,4096]{1,0:T(8,128)(2,1)} %bitcast.5, f32[1,4352]{1,0:T(1,128)S(1)} %broadcast_in_dim.6.table, bf16[512,2048]{1,0:T(8,128)(2,1)} %qw.1, bf16[512,512]{1,0:T(8,128)(2,1)} %kw.1, bf16[512,512]{1,0:T(8,128)(2,1)} %vw.1), custom_call_target="tpu_custom_call" | custom-call | tf_op jit(solution)/shard_map/pallas_call | solution.py:563
  73.5 0.8 %copy.8 = bf16[1,128,2048]{2,1,0:T(8,128)(2,1)} copy(bf16[1,128,2048]{2,1,0:T(8,128)(2,1)S(1)} %bitcast.4) | data formatting | bytes 1048576
  (2 shorter events, 0.0 us)

commit v4 on v3

--- a/solution.py
+++ b/solution.py
@@ -112,7 +112,7 @@
 
 
 def kernel(tok_in, table, qw, kw, vw, out,
-           tok, rq, rk, rv, tq, csq, wkv, wq, kb, vb, qt, acc, top, proj, sbuf, osend, obuf,
+           tok, gain, rq, rk, rv, tq, csq, wkv, wq, kb, vb, qt, acc, top, proj, sbuf, osend, obuf,
            tok_s, loc_s, zs, zr, ws, wr, ts, tr, fs, fr,
            s_a, r_a, x_a, s_b, r_b, x_b, s_c, r_c, x_c, s_d, r_d, x_d, os_, or_, outs_):
     c, f = lax.axis_index("ctx"), lax.axis_index("fsdp")
@@ -164,9 +164,11 @@
         line = pl.ds(pl.multiple_of(i * 16, 16), 16)
         values = tok[line, :].astype(F32)
         inverse = lax.rsqrt(jnp.mean(values * values, axis=-1, keepdims=True) + EPS)
-        tq[k, line, :] = (values * inverse * table[:, 0:4096]).astype(BF16)
+        tq[k, line, :] = (values * inverse * gain[...]).astype(BF16)
         return 0
 
+    for i in range(32):
+        gain[:, i * 128:i * 128 + 128] = table[i:i + 1, :]
     for copy in staged:
         copy.wait()
 
@@ -202,9 +204,9 @@
         copy.wait()
         lax.fori_loop(i * 4, i * 4 + 4, norm_rows, 0)
     step_in = lax.broadcasted_iota(jnp.int32, (128, 128), 0)
-    place = table[:, 4096:4224]
+    place = table[32:33, :]
     column = jnp.where(step_in < 64, place[:, 0:1], place[:, 64:65]) + lax.rem(step_in, 64).astype(F32)
-    angles = column * table[:, 4224:4352]
+    angles = column * table[33:34, :]
     first_half = lax.broadcasted_iota(jnp.int32, (128, 128), 1) < 64
     csq[k, 0:128, :] = jnp.where(first_half, jnp.cos(angles), jnp.sin(angles))
     csq[k, 128:136, :] = jnp.broadcast_to(place, (8, 128))
@@ -555,7 +557,8 @@
 
 def on_device(tokens, positions, norm_gain, query_weight, key_weight, value_matrix):
     frequency = BASE ** (-(jnp.arange(HEAD // 2, dtype=F32) * 2.0) / HEAD)
-    table = jnp.concatenate([norm_gain, positions[0].astype(F32), frequency, frequency])[None, :]
+    lines = [norm_gain.reshape(32, HEAD), positions.astype(F32), jnp.concatenate([frequency, frequency])[None, :]]
+    table = jnp.concatenate(lines, axis=0)
     vmem = pl.BlockSpec(memory_space=pltpu.VMEM)
     anywhere = pl.BlockSpec(memory_space=pl.ANY)
     far = pl.BlockSpec(memory_space=pltpu.HBM)
@@ -567,6 +570,7 @@
         out_specs=anywhere,
         scratch_shapes=[
             pltpu.VMEM((128, 4096), BF16),
+            pltpu.VMEM((1, 4096), F32),
             pltpu.VMEM((32, 2048), BF16),
             pltpu.VMEM((32, 512), BF16),
             pltpu.VMEM((32, 512), BF16),

time: 74.5 us -> 74.2 us (level)
  local copies, waits for them, and re-layouts: 1.6 us -> 0.8 us
  other arithmetic: 0.67 us -> 1.47 us
    concatenate x1 -> x0, local copies, waits for them, and re-layouts: 0.8 us -> none  [on_device(): jnp.concatenate([norm_gain, positions[0].astype(F32), frequency, frequency])]
where the time goes in v4:
time: 74.2 us; the launch traced here: 74.1 us
  Pallas kernels  71.8 us (97%)
  other arithmetic  1.47 us (2%)
  local copies, waits for them, and re-layouts  0.8 us (1%)
    pallas_call x1, Pallas kernels, on_device(): pl.pallas_call(kernel, out_shape=jax.ShapeDtypeStruct((128, 2048), BF16),...  71.8 us

profile of v4, /device:TPU:1, one launch (start us, length us, event | category | flops | bytes accessed | tf_op | source)
XLA Modules:
  0.0 74.1 jit_solution(4455726135980291038)
XLA Ops:
  0.0 0.7 convert_element_type.3
  0.7 0.1 maximum_bitcast_fusion
  0.7 0.7 pad_maximum_fusion.table
  1.5 71.8 %shard_map.64 = bf16[128,2048]{1,0:T(8,128)(2,1)S(1)} custom-call(bf16[128,4096]{1,0:T(8,128)(2,1)} %bitcast.6, f32[34,128]{1,0:T(8,128)S(1)} %pad_maximum_fusion.table, bf16[512,2048]{1,0:T(8,128)(2,1)} %qw.1, bf16[512,512]{1,0:T(8,128)(2,1)} %kw.1, bf16[512,512]{1,0:T(8,128)(2,1)} %vw.1), custom_call_target="tpu_custom_call" | custom-call | tf_op jit(solution)/shard_map/pallas_call | solution.py:566
  73.3 0.8 %copy.8 = bf16[1,128,2048]{2,1,0:T(8,128)(2,1)} copy(bf16[1,128,2048]{2,1,0:T(8,128)(2,1)S(1)} %bitcast.5) | data formatting | bytes 1048576
  (1 shorter events, 0.0 us)
